TPU v7x, 32 devices: a whole 2x2x4 slice. The times are simulated.
32 devices in a mesh: group: 2 (over x), dp: 2 (over core), tensor: 8 (over z, y).
Axes of the slice: x: 2, y: 2, z: 4, core: 2. Of those that a mesh axis runs over, the one named last changes fastest.
Arguments:
- teacher_hidden: bfloat16 [1024, 8192], P(('group', 'dp'), 'tensor'), may hold values from -6 to 6
- teacher_gain: float32 [8192], P('tensor'), may hold values from 0.1 to 1.9
- project_weight: bfloat16 [8192, 3584], P('tensor'), may hold values from -0.0625 to 0.0625
- student_hidden: bfloat16 [1024, 3584], P(('group', 'dp', 'tensor')), may hold values from -6 to 6
- student_gain: float32 [3584], replicated, may hold values from 0.1 to 1.9
- gate_weight: bfloat16 [3584, 9472], P(('group', 'dp'), 'tensor'), may hold values from -0.09375 to 0.09375
- up_weight: bfloat16 [3584, 9472], P(('group', 'dp'), 'tensor'), may hold values from -0.09375 to 0.09375
- down_weight: bfloat16 [9472, 3584], P('tensor', ('group', 'dp')), may hold values from -0.0625 to 0.0625
- owner_map: int32 [64, 1], P(('group', 'dp')), may hold values from 0 to 3; in each aligned block of 16 rows (0 to 15, 16 to 31, ...) at most 8 rows name the same one
- token_ids: int32 [1024], P(('group', 'dp', 'tensor')), may hold values from 0 to 511
- token_counts: int32 [64], P(('group', 'dp')), may hold values from 1 to 16
- id_weight: float32 [512], replicated, may hold values from 0.25 to 4
Outputs:
- student_out: bfloat16 [4, 16, 32, 3584], P(('group', 'dp'), 'tensor')
- down_grad: float32 [3584, 9472], P(('group', 'dp'), 'tensor')
Inputs may be any that keep to these rules, and one draw needn't show every extreme that they name: `owner_map`: of the 16 episodes of one index of group and dp (aligned blocks of 16 rows), at most 8 have the same owner; owner o is index o of group and dp in mesh order.
All inputs are finite; a program needn't handle non-finite values.
Results may differ from a plain program's by a relative error of at most 0.02.
Values may be sent and summed in bfloat16 or wider, within the bound.
A program may use at most 128 MiB of HBM per device.

v0:
```python
import math

import jax
import jax.numpy as jnp
from jax import lax
from jax.sharding import PartitionSpec as P

EP_LEN = 16
EXTRA = 128
EPSILON = 1e-06
OWNER_AXES = ("group", "dp")


def exchange(blocks):
    return lax.all_to_all(blocks, OWNER_AXES, split_axis=0, concat_axis=0, tiled=True)


def by_columns(rows, owners):
    return rows.reshape(rows.shape[0], owners, -1).transpose(1, 0, 2)


def three_terms(values):
    high = lax.reduce_precision(values, 8, 7)
    rest = values - high
    middle = lax.reduce_precision(rest, 8, 7)
    return high, middle, rest - middle


def build_selector(owner_list, owners, capacity):
    onehot = (owner_list[:, :, None] == jnp.arange(owners, dtype=jnp.int32)).astype(jnp.int32)
    earlier = jnp.cumsum(onehot, axis=1) - onehot
    rank_list = jnp.sum(earlier * onehot, axis=2)
    target = owner_list * capacity + rank_list
    slots = jnp.arange(owners * capacity, dtype=jnp.int32)
    return (target[:, None, :] == slots[None, :, None]).astype(jnp.bfloat16)


def local(
    teacher_hidden,
    teacher_gain,
    project_weight,
    student_hidden,
    student_gain,
    gate_weight,
    up_weight,
    down_weight,
    owner_map,
    token_ids,
    token_counts,
    id_weight,
):
    owners = lax.axis_size("group") * lax.axis_size("dp")
    tensors = lax.axis_size("tensor")
    tensor_index = lax.axis_index("tensor")
    owner_index = lax.axis_index(OWNER_AXES)
    episodes = token_counts.shape[0]
    own_span = EP_LEN // tensors
    share = own_span * episodes
    capacity = max(2, 2 * episodes // owners)
    received = owners * capacity
    student_width = student_hidden.shape[1]
    width = student_width // owners
    tokens_all = EP_LEN * episodes * owners
    teacher_width = teacher_hidden.shape[1] * tensors

    id_rows = token_ids.reshape(own_span, episodes)
    looked = jnp.sum(
        jnp.where(
            id_rows[:, :, None] == jnp.arange(id_weight.shape[0], dtype=jnp.int32)[None, None, :],
            id_weight[None, None, :],
            0.0,
        ),
        axis=2,
    )
    position = tensor_index * own_span + jnp.arange(own_span, dtype=jnp.int32)[:, None]
    token_weight = jnp.where(position < token_counts[None, :], looked, 0.0).reshape(share, 1)

    own_rows = student_hidden.astype(jnp.float32)
    own_rescale = lax.rsqrt(jnp.mean(own_rows * own_rows, axis=1, keepdims=True) + EPSILON)
    owner_rows = jnp.tile(owner_map.astype(jnp.float32), (own_span, 1))
    extras = jnp.concatenate([token_weight, owner_rows, *three_terms(own_rescale)], axis=1)
    extras = jnp.pad(extras, ((0, 0), (0, EXTRA - extras.shape[1]))).astype(jnp.bfloat16)
    arrived = exchange(
        jnp.concatenate(
            [
                by_columns(student_hidden, owners),
                jnp.broadcast_to(extras[None], (owners, share, EXTRA)),
            ],
            axis=2,
        )
    )
    rows = owners * share
    student_block = arrived[:, :, :width].reshape(rows, width).astype(jnp.float32)
    facts = arrived[:, :, width:].astype(jnp.float32)
    weight_rows = facts[:, :, 0].reshape(rows, 1)
    owner_list = facts[:, :episodes, 1].astype(jnp.int32)
    rescale = (facts[:, :, 2] + facts[:, :, 3] + facts[:, :, 4]).reshape(rows, 1)
    gain = lax.dynamic_slice_in_dim(student_gain, owner_index * width, width, 0)
    normed = (student_block * rescale * gain[None, :]).astype(jnp.bfloat16)
    gathered = lax.all_gather(normed, "tensor", axis=0, tiled=True)

    widened = teacher_hidden.astype(jnp.float32)
    squares = jnp.sum(widened * widened, axis=1)
    scaled = (widened * teacher_gain[None, :]).astype(jnp.bfloat16)
    inverse = lax.rsqrt(lax.psum(squares, "tensor") / teacher_width + EPSILON)
    summed = lax.psum_scatter(
        jnp.dot(scaled, project_weight, preferred_element_type=jnp.float32).astype(jnp.bfloat16),
        "tensor",
        scatter_dimension=0,
        tiled=True,
    ).astype(jnp.float32)
    own_inverse = lax.dynamic_slice_in_dim(inverse, tensor_index * share, share, 0)
    projected = exchange(by_columns((summed * own_inverse[:, None]).astype(jnp.bfloat16), owners))

    hidden = gate_weight.shape[1]
    gate_part = jnp.dot(gathered, gate_weight, preferred_element_type=jnp.float32)
    up_part = jnp.dot(gathered, up_weight, preferred_element_type=jnp.float32)
    parts = jnp.stack(
        [
            gate_part.astype(jnp.bfloat16).reshape(owners, -1, hidden),
            up_part.astype(jnp.bfloat16).reshape(owners, -1, hidden),
        ],
        axis=1,
    )
    sums = lax.psum_scatter(parts, OWNER_AXES, scatter_dimension=0, tiled=True).astype(jnp.float32)
    activated = (jax.nn.silu(sums[0, 0]) * sums[0, 1]).astype(jnp.bfloat16)
    act_all = lax.all_gather(activated, OWNER_AXES, axis=0, tiled=True)
    branch = jnp.dot(act_all, down_weight, preferred_element_type=jnp.float32)
    branch_local = lax.psum_scatter(
        branch.astype(jnp.bfloat16), "tensor", scatter_dimension=0, tiled=True
    ).astype(jnp.float32)
    predicted = student_block + branch_local

    difference = predicted - projected.reshape(rows, width).astype(jnp.float32)
    grad_block = (weight_rows * difference * (1.0 / math.sqrt(tokens_all))).astype(jnp.bfloat16)
    grad_all = lax.all_gather(grad_block, "tensor", axis=0, tiled=True)
    down_grad = jnp.einsum("rc,rh->ch", grad_all, act_all, preferred_element_type=jnp.float32)

    selector = build_selector(owner_list, owners, capacity)
    picked = jnp.einsum(
        "sre,spef->sprf",
        selector,
        predicted.astype(jnp.bfloat16).reshape(owners, own_span, episodes, width),
        preferred_element_type=jnp.float32,
    ).astype(jnp.bfloat16)
    outgoing = picked.reshape(owners, own_span, owners, capacity, width).transpose(2, 1, 0, 3, 4)
    incoming = exchange(outgoing.reshape(owners, own_span, received, width))
    student_out = incoming.transpose(1, 2, 0, 3).reshape(1, own_span, received, student_width)
    return (student_out, down_grad)


def solution(mesh):
    in_specs = (
        P(("group", "dp"), "tensor"),
        P("tensor"),
        P("tensor", None),
        P(("group", "dp", "tensor"), None),
        P(),
        P(("group", "dp"), "tensor"),
        P(("group", "dp"), "tensor"),
        P("tensor", ("group", "dp")),
        P(("group", "dp"), None),
        P(("group", "dp", "tensor")),
        P(("group", "dp")),
        P(),
    )
    out_specs = (P(("group", "dp"), "tensor", None, None), P(("group", "dp"), "tensor"))
    return jax.shard_map(local, mesh=mesh, in_specs=in_specs, out_specs=out_specs, check_vma=False)
```

profile of v0, /device:TPU:0, one launch (start us, length us, event | category | flops | bytes accessed | tf_op | source)
XLA Modules:
  0.0 378.6 jit_solution(4953372782439392148)
XLA Ops:
  7.2 1.2 multiply_reduce_fusion
  8.4 1.0 reshape.158
  9.4 0.7 eq.43
  10.2 0.8 select_reduce_fusion
  11.0 0.7 fusion.19
  11.8 0.1 select_n.26
  11.9 0.7 convert_bitcast_fusion
  12.5 0.1 tile.13
  12.6 0.1 copy.50
  12.8 0.7 pad_maximum_fusion.1
  13.5 4.2 %all-to-all-start = ((bf16[4,32,1024]{2,1,0:T(8,128)(2,1)}), bf16[4,32,1024]{2,1,0:T(8,128)(2,1)S(1)}, u32[]{:S(2)}, u32[]{:S(2)}) async-start(bf16[4,32,1024]{2,1,0:T(8,128)(2,1)} %pad_maximum_fusion.1), calls=%async_computation | async-start | bytes 524288 | tf_op jit(solution)/shard_map/all_to_all | solution.py:15
  17.8 0.8 dynamic_slice.6
  18.6 5.2 %all-to-all-done = bf16[4,32,1024]{2,1,0:T(8,128)(2,1)S(1)} async-done(((bf16[4,32,1024]{2,1,0:T(8,128)(2,1)}), bf16[4,32,1024]{2,1,0:T(8,128)(2,1)S(1)}, u32[]{:S(2)}, u32[]{:S(2)}) %all-to-all-start) | async-done | bytes 262176 | tf_op jit(solution)/shard_map/all_to_all | solution.py:15
  23.8 0.2 slice_reduce_fusion
  24.1 0.8 fusion.8
  25.0 47.4 %all-gather.4.cloned.1.call-done = bf16[1024,896]{1,0:T(8,128)(2,1)} async-done(((bf16[128,896]{1,0:T(8,128)(2,1)}), bf16[1024,896]{1,0:T(8,128)(2,1)}) %all-gather.4.cloned.1.call-update) | async-done | bytes 1835024 | tf_op jit(solution)/shard_map/all_gather | solution.py:100
  72.4 5.5 %convolution_convert_fusion.2 = bf16[1024,1184]{0,1:T(8,128)(2,1)} fusion(bf16[1024,896]{1,0:T(8,128)(2,1)} %all-gather.4.cloned.1.call-done, bf16[896,1184]{0,1:T(8,128)(2,1)S(1)} %copy-done), kind=kOutput, calls=%fused_computation.3 | convolution fusion | flops 2173861888 | bytes 6381568 | tf_op jit(solution)/shard_map/dot_general | solution.py:116
  77.9 5.7 %stack_reshape.6 = bf16[4,1,256,1184]{2,0,3,1:T(4,128)(2,1)} reshape(bf16[1024,1184]{0,1:T(8,128)(2,1)} %convolution_convert_fusion.2) | data formatting | bytes 4849664 | tf_op jit(solution)/shard_map/stack;reshape | solution.py:118
  83.6 3.6 copy.44
  87.2 4.0 %convolution_convert_fusion.1 = bf16[1024,1184]{0,1:T(8,128)(2,1)} fusion(bf16[1024,896]{1,0:T(8,128)(2,1)S(1)} %copy-done.4, bf16[896,1184]{0,1:T(8,128)(2,1)S(1)} %copy-done.3), kind=kOutput, calls=%fused_computation.2 | convolution fusion | flops 2173861888 | bytes 6381568 | tf_op jit(solution)/shard_map/dot_general | solution.py:117
  91.2 5.7 %stack_reshape.7 = bf16[4,1,256,1184]{2,0,3,1:T(4,128)(2,1)} reshape(bf16[1024,1184]{0,1:T(8,128)(2,1)} %convolution_convert_fusion.1) | data formatting | bytes 4849664 | tf_op jit(solution)/shard_map/stack;reshape | solution.py:118
  96.9 2.1 copy.45
  99.0 0.3 copy-done.1
  99.3 2.6 pad_maximum_fusion
  102.0 47.6 %reduce-scatter.4.cloned.1.call-done = bf16[1,2,256,1184]{2,3,1,0:T(8,128)(2,1)} async-done(((bf16[4,2,256,1184]{2,3,1,0:T(8,128)(2,1)}), bf16[1,2,256,1184]{2,3,1,0:T(8,128)(2,1)}) %reduce-scatter.4.cloned.1.call-update) | async-done | bytes 1212432 | tf_op jit(solution)/shard_map/reduce_scatter | solution.py:125
  149.6 1.4 convert_element_type.93
  151.1 1.2 fusion.2
  152.3 6.4 %convolution_convert_fusion = bf16[256,3584]{1,0:T(8,128)(2,1)} fusion(bf16[1024,3584]{1,0:T(8,128)(2,1)} %param.14, bf16[256,1024]{1,0:T(8,128)(2,1)S(1)} %copy-done.2, f32[1024]{0:T(1024)S(1)} %copy-done.5), kind=kOutput, calls=%fused_computation | convolution fusion | flops 1880752128 | bytes 9703424 | tf_op jit(solution)/shard_map/dot_general | solution.py:107
  158.8 18.4 %all-gather.6.cloned.1.call-done = bf16[1024,1184]{0,1:T(8,128)(2,1)} async-done(((bf16[256,1184]{0,1:T(8,128)(2,1)}), bf16[1024,1184]{0,1:T(8,128)(2,1)}) %all-gather.6.cloned.1.call-update) | async-done | bytes 2424848 | tf_op jit(solution)/shard_map/all_gather | solution.py:127
  177.1 6.5 %convolution_convert_fusion.3 = bf16[1024,896]{1,0:T(8,128)(2,1)} fusion(bf16[1024,1184]{0,1:T(8,128)(2,1)} %all-gather.6.cloned.1.call-done, bf16[1184,896]{1,0:T(8,128)(2,1)} %param.19), kind=kOutput, calls=%fused_computation.4 | convolution fusion | flops 2173566976 | bytes 6381568 | tf_op jit(solution)/shard_map/dot_general | solution.py:128
  183.7 0.2 fusion.4
  183.8 21.4 %psum.7 = f32[256]{0:T(256)S(1)} all-reduce(f32[256]{0:T(256)S(1)} %fusion.4), channel_id=1, replica_groups=mesh['group'=2,'dp'=2,'tensor'=8] {'tensor'}, use_global_device_ids=true, to_apply=%region_8.9 | all-reduce | flops 256 | bytes 2048 | tf_op jit(solution)/shard_map/psum | solution.py:105
  205.3 41.9 %reduce-scatter.8.cloned.1.call-done = bf16[32,3584]{1,0:T(8,128)(2,1)} async-done(((bf16[256,3584]{1,0:T(8,128)(2,1)}), bf16[32,3584]{1,0:T(8,128)(2,1)}) %reduce-scatter.8.cloned.1.call-update) | async-done | bytes 229392 | tf_op jit(solution)/shard_map/reduce_scatter | solution.py:106
  247.2 1.0 multiply_convert_fusion
  248.3 0.7 copy.55
  249.0 3.4 all-to-all-start.2
  252.4 0.2 all-gather.8.cloned.1.call-start
  252.7 5.3 %all-to-all-done.2 = bf16[4,32,896]{2,1,0:T(8,128)(2,1)S(1)} async-done(((bf16[4,32,896]{2,1,0:T(8,128)(2,1)}), bf16[4,32,896]{2,1,0:T(8,128)(2,1)S(1)}, u32[]{:S(2)}, u32[]{:S(2)}) %all-to-all-start.2) | async-done | bytes 229408 | tf_op jit(solution)/shard_map/all_to_all | solution.py:15
  258.0 58.9 %reduce-scatter.6.cloned.1.call-done = bf16[128,896]{1,0:T(8,128)(2,1)} async-done(((bf16[1024,896]{1,0:T(8,128)(2,1)}), bf16[128,896]{1,0:T(8,128)(2,1)}) %reduce-scatter.6.cloned.1.call-update) | async-done | bytes 229392 | tf_op jit(solution)/shard_map/reduce_scatter | solution.py:129
  316.8 1.8 fusion.11
  318.6 0.3 fusion.17
  319.0 0.2 select_reduce_fusion.1
  319.3 0.4 fusion
  319.7 10.6 %all_to_all.15 = bf16[4,2,32,896]{3,2,1,0:T(8,128)(2,1)S(1)} all-to-all(bf16[4,2,32,896]{3,2,1,0:T(8,128)(2,1)S(1)} %bitcast.65), channel_id=1, replica_groups=mesh['group'=2,'dp'=2,'tensor'=8] {'group','dp'}, dimensions={0} | all-to-all | bytes 917504 | tf_op jit(solution)/shard_map/all_to_all | solution.py:15
  330.3 0.4 copy.47
  330.7 0.9 reshape.162
  331.6 33.1 %all-gather.8.cloned.1.call-done = bf16[1024,896]{1,0:T(8,128)(2,1)} async-done(((bf16[128,896]{1,0:T(8,128)(2,1)}), bf16[1024,896]{1,0:T(8,128)(2,1)}) %all-gather.8.cloned.1.call-update) | async-done | bytes 1835024 | tf_op jit(solution)/shard_map/all_gather | solution.py:136
  364.8 6.9 %fusion.21 = f32[896,1184]{0,1:T(8,128)} fusion(bf16[1024,1184]{0,1:T(8,128)(2,1)} %all-gather.6.cloned.1.call-done, bf16[1024,896]{1,0:T(8,128)(2,1)} %all-gather.8.cloned.1.call-done), kind=kOutput, calls=%fused_computation.57 | convolution fusion | flops 2172649472 | bytes 8503296 | tf_op jit(solution)/shard_map/rc,rh->ch/dot_general | solution.py:137
  (39 shorter events, 0.8 us)
Async XLA Ops:
  7.2 65.3 %copy-start = (bf16[896,1184]{0,1:T(8,128)(2,1)S(1)}, bf16[896,1184]{0,1:T(8,128)(2,1)}, u32[]{:S(2)}) copy-start(bf16[896,1184]{0,1:T(8,128)(2,1)} %param.17) | copy-start | bytes 6365188
  13.5 10.2 %all-to-all-start = ((bf16[4,32,1024]{2,1,0:T(8,128)(2,1)}), bf16[4,32,1024]{2,1,0:T(8,128)(2,1)S(1)}, u32[]{:S(2)}, u32[]{:S(2)}) async-start(bf16[4,32,1024]{2,1,0:T(8,128)(2,1)} %pad_maximum_fusion.1), calls=%async_computation | async-start | bytes 524288 | tf_op jit(solution)/shard_map/all_to_all | solution.py:15
  17.8 54.7 %all-gather.4.cloned.1.call-start = ((), (), s32[]{:S(2)}) async-start(), calls=%async_computation.6 | async-start | bytes 2064384 | tf_op jit(solution)/shard_map/all_gather | solution.py:100
  25.0 124.6 %reduce-scatter.4.cloned.1.call-start = ((), (), s32[]{:S(2)}) async-start(), calls=%async_computation.7 | async-start | bytes 6062080 | tf_op jit(solution)/shard_map/reduce_scatter | solution.py:125
  83.6 3.6 copy-start.3
  83.6 3.6 copy-start.4
  96.9 2.4 copy-start.1
  101.9 75.2 %all-gather.6.cloned.1.call-start = ((), (), s32[]{:S(2)}) async-start(), calls=%async_computation.8 | async-start | bytes 3031040 | tf_op jit(solution)/shard_map/all_gather | solution.py:127
  151.0 1.3 copy-start.2
  151.1 1.3 copy-start.5
  152.3 94.9 %reduce-scatter.8.cloned.1.call-start = ((), (), s32[]{:S(2)}) async-start(), calls=%async_computation.10 | async-start | bytes 2064384 | tf_op jit(solution)/shard_map/reduce_scatter | solution.py:106
  158.7 158.1 %reduce-scatter.6.cloned.1.call-start = ((), (), s32[]{:S(2)}) async-start(), calls=%async_computation.9 | async-start | bytes 2064384 | tf_op jit(solution)/shard_map/reduce_scatter | solution.py:129
  249.0 9.0 %all-to-all-start.2 = ((bf16[4,32,896]{2,1,0:T(8,128)(2,1)}), bf16[4,32,896]{2,1,0:T(8,128)(2,1)S(1)}, u32[]{:S(2)}, u32[]{:S(2)}) async-start(bf16[4,32,896]{2,1,0:T(8,128)(2,1)} %bitcast.64), calls=%async_computation.5 | async-start | bytes 458752 | tf_op jit(solution)/shard_map/all_to_all | solution.py:15
  252.4 112.4 %all-gather.8.cloned.1.call-start = ((), (), s32[]{:S(2)}) async-start(), calls=%async_computation.11 | async-start | bytes 2064384 | tf_op jit(solution)/shard_map/all_gather | solution.py:136
Sparse Core Ops, SparseCore 0:
  25.1 47.3 all-gather.3
  102.0 47.4 reduce-scatter.3
  152.4 24.7 all-gather.5
  180.5 66.7 reduce-scatter.7
  251.1 65.6 reduce-scatter.5
  319.5 45.2 all-gather.7
where the time goes:
time: 379 us
  waiting for transfers between devices  258 us (68%)
  blocking collectives  32 us (8%)
  matrix products  29.6 us (8%)
  local copies, waits for them, and re-layouts  22.6 us (6%)
  between operations  14.3 us (4%)
  other arithmetic  14.1 us (4%)
  starting transfers between devices  8.01 us (2%)
    reduce_scatter x1, waiting for transfers between devices, local(): lax.psum_scatter(branch.astype(jnp.bfloat16), 'tensor', scatter_dimension...  58.9 us
    reduce_scatter x1, waiting for transfers between devices, local(): lax.psum_scatter(parts, OWNER_AXES, scatter_dimension=0, tiled=True)  47.6 us
    all_gather x1, waiting for transfers between devices, local(): gathered = lax.all_gather(normed, 'tensor', axis=0, tiled=True)  47.4 us
    reduce_scatter x1, waiting for transfers between devices, local(): lax.psum_scatter(jnp.dot(scaled, project_weight, preferred_element_type=j...  41.9 us
    all_gather x1, waiting for transfers between devices, local(): grad_all = lax.all_gather(grad_block, 'tensor', axis=0, tiled=True)  33.1 us
    psum x1, blocking collectives, local(): inverse = lax.rsqrt(lax.psum(squares, 'tensor') / teacher_width + EPSILON)  21.4 us
    all_gather x1, waiting for transfers between devices, local(): act_all = lax.all_gather(activated, OWNER_AXES, axis=0, tiled=True)  18.4 us
    another operation x4, local copies, waits for them, and re-layouts, local(): jnp.stack([gate_part.astype(jnp.bfloat16).reshape(owners, -1, hidden), up...  17.2 us
  transfers between devices with their start and end apart: 8, of which 8 were waited for; matrix products, arithmetic and copies ran while one was open for 5% of the time, Pallas kernels for 0%

commit v1 on v0

--- a/solution.py
+++ b/solution.py
@@ -1,8 +1,11 @@
+import functools
 import math
 
 import jax
 import jax.numpy as jnp
 from jax import lax
+from jax.experimental import pallas as pl
+from jax.experimental.pallas import tpu as pltpu
 from jax.sharding import PartitionSpec as P
 
 EP_LEN = 16
@@ -35,7 +38,7 @@
     return (target[:, None, :] == slots[None, :, None]).astype(jnp.bfloat16)
 
 
-def local(
+def general(
     teacher_hidden,
     teacher_gain,
     project_weight,
@@ -149,6 +152,679 @@
     return (student_out, down_grad)
 
 
+MESH = pl.DeviceIdType.MESH
+TILE = 256
+
+
+def over_tiles(width, body):
+    whole = width // TILE
+
+    def step(index, carry):
+        body(pl.multiple_of(index * TILE, TILE), TILE)
+        return carry
+
+    if whole:
+        lax.fori_loop(0, whole, step, 0)
+    if width > whole * TILE:
+        body(whole * TILE, width - whole * TILE)
+
+
+def column_of(row, eye):
+    return jnp.sum(jnp.where(eye, row, 0.0), axis=1, keepdims=True)
+
+
+def fused_kernel(
+    size,
+    teacher_ref,
+    teacher_gain_ref,
+    project_ref,
+    student_ref,
+    student_gain_ref,
+    gate_ref,
+    up_ref,
+    down_ref,
+    owner_ref,
+    ids_ref,
+    counts_ref,
+    id_weight_ref,
+    grad_out,
+    act_out,
+    student_out,
+    th,
+    scaled,
+    pw,
+    tp,
+    st,
+    nrm,
+    gw,
+    uw,
+    dw,
+    nb,
+    own_part,
+    d2s,
+    d2r,
+    own_x,
+    xs,
+    xr,
+    act,
+    bp0,
+    rss,
+    rsr,
+    trs,
+    trr,
+    sqs,
+    sqr,
+    inverse_ref,
+    pjs,
+    pj,
+    sb,
+    ext,
+    ga,
+    predb,
+    sos,
+    so,
+    load_sem,
+    nx_s,
+    nx_r,
+    raw_s,
+    raw_r,
+    ext_s,
+    ext_r,
+    pj_s,
+    pj_r,
+    so_s,
+    so_r,
+    sq_s,
+    sq_r,
+    ag_s,
+    ag_r,
+    tr_s,
+    tr_r,
+    rs_s,
+    rs_r,
+    gg_s,
+    gg_r,
+    d2_s,
+    d2_r,
+    x_s,
+    x_r,
+    a1_s,
+    a1_r,
+    a2_s,
+    a2_r,
+    a3_s,
+    a3_r,
+    out_sem,
+):
+    T, O, E, span, cap = size["T"], size["O"], size["E"], size["span"], size["cap"]
+    share = span * E
+    rows = O * share
+    half, quarter = rows // 2, rows // 4
+    W = nb.shape[2]
+    H = gw.shape[1]
+    DS = st.shape[1]
+    t_half = share // 2
+    f32, bf16 = jnp.float32, jnp.bfloat16
+
+    x = lax.axis_index("group")
+    c = lax.axis_index("dp")
+    t = lax.axis_index("tensor")
+    o = x * 2 + c
+    odd = lax.rem(t, 2)
+    r = (1 - odd) * lax.div(t, 2) + odd * (T - 1 - lax.div(t, 2))
+
+    def at_ring(position):
+        p = lax.rem(position, T)
+        upper = lax.div(p, T // 2)
+        return (1 - upper) * (2 * p) + upper * (2 * (T - 1 - p) + 1)
+
+    nxt, prv = at_ring(r + 1), at_ring(r + T - 1)
+    peers = (
+        (1 - x, c, {"group": 1 - x}),
+        (1 - x, 1 - c, {"group": 1 - x, "dp": 1 - c}),
+        (x, 1 - c, {"dp": 1 - c}),
+    )
+    other_chip, core_peer = {"group": 1 - x}, {"dp": 1 - c}
+
+    def remote(src, dst, send, recv, device):
+        return pltpu.make_async_remote_copy(
+            src_ref=src, dst_ref=dst, send_sem=send, recv_sem=recv, device_id=device, device_id_type=MESH
+        )
+
+    loads = [
+        pltpu.make_async_copy(src, dst, load_sem.at[index])
+        for index, (src, dst) in enumerate(
+            [(student_ref, st), (teacher_ref, th), (project_ref, pw), (gate_ref, gw), (up_ref, uw), (down_ref, dw)]
+        )
+    ]
+    for load in loads:
+        load.start()
+
+    barrier = pltpu.get_barrier_semaphore()
+    for _, _, device in peers:
+        pl.semaphore_signal(barrier, inc=1, device_id=device, device_id_type=MESH)
+    for step in range(1, T):
+        pl.semaphore_signal(barrier, inc=1, device_id={"tensor": at_ring(r + step)}, device_id_type=MESH)
+
+    def columns(owner):
+        return pl.ds(pl.multiple_of(owner * W, W), W)
+
+    def owner_rows(owner):
+        return pl.ds(pl.multiple_of(owner * share, share), share)
+
+    def nx(k):
+        return remote(
+            nrm.at[:, columns(peers[k][0] * 2 + peers[k][1])],
+            nb.at[0, owner_rows(o), :],
+            nx_s.at[k],
+            nx_r.at[k],
+            peers[k][2],
+        )
+
+    def raw(k):
+        return remote(
+            st.at[:, columns(peers[k][0] * 2 + peers[k][1])],
+            sb.at[owner_rows(o), :],
+            raw_s.at[k],
+            raw_r.at[k],
+            peers[k][2],
+        )
+
+    def extra(k):
+        return remote(ext.at[o], ext.at[o], ext_s.at[k], ext_r.at[k], peers[k][2])
+
+    def proj(k):
+        return remote(
+            pjs.at[:, columns(peers[k][0] * 2 + peers[k][1])],
+            pj.at[owner_rows(o), :],
+            pj_s.at[k],
+            pj_r.at[k],
+            peers[k][2],
+        )
+
+    out_rows = span * O * cap
+
+    def outgoing(k):
+        q = peers[k][0] * 2 + peers[k][1]
+        return remote(
+            sos.at[pl.ds(pl.multiple_of(q * out_rows, out_rows), out_rows), :],
+            so.at[:, columns(o)],
+            so_s.at[k],
+            so_r.at[k],
+            peers[k][2],
+        )
+
+    def block_rows(position):
+        return pl.ds(pl.multiple_of(at_ring(position) * share, share), share)
+
+    def squares(step):
+        return remote(
+            sqs.at[block_rows(r + step), :],
+            sqr.at[step],
+            sq_s.at[step],
+            sq_r.at[step],
+            {"tensor": at_ring(r + step)},
+        )
+
+    def to(d):
+        return {"tensor": nxt if d == 0 else prv}
+
+    def part(d, n):
+        return pl.ds(d * n, n)
+
+    def ag(d, g):
+        return remote(
+            nb.at[g - 1, part(d, half), :], nb.at[g, part(d, half), :], ag_s.at[d, g], ag_r.at[d, g], to(d)
+        )
+
+    def rs(d, g):
+        return remote(
+            rss.at[g, part(d, half), :], rsr.at[g, part(d, half), :], rs_s.at[d, g], rs_r.at[d, g], to(d)
+        )
+
+    def tr(d, k):
+        return remote(
+            trs.at[k, part(d, t_half), :], trr.at[k, part(d, t_half), :], tr_s.at[d, k], tr_r.at[d, k], to(d)
+        )
+
+    def gg(s, g):
+        d = s * 2 // O
+        return remote(
+            ga.at[g - 1, part(s, share), :], ga.at[g, part(s, share), :], gg_s.at[s, g], gg_r.at[s, g], to(d)
+        )
+
+    def d2(g):
+        return remote(d2s.at[g], d2r.at[g], d2_s.at[g], d2_r.at[g], core_peer)
+
+    def xch(g):
+        return remote(xs.at[g], xr.at[g], x_s.at[g], x_r.at[g], other_chip)
+
+    def act_rows(core, chip):
+        return pl.ds(pl.multiple_of((core * 2 + chip) * quarter, quarter), quarter)
+
+    own_act = act_rows(c, x)
+    far_act = act_rows(c, 1 - x)
+
+    def a1(g):
+        return remote(act.at[g, own_act, :], act.at[g, own_act, :], a1_s.at[g], a1_r.at[g], other_chip)
+
+    def a2(g):
+        return remote(act.at[g, own_act, :], act.at[g, own_act, :], a2_s.at[g], a2_r.at[g], core_peer)
+
+    def a3(g):
+        return remote(act.at[g, far_act, :], act.at[g, far_act, :], a3_s.at[g], a3_r.at[g], core_peer)
+
+    loads[0].wait()
+    wide = st[...].astype(f32)
+    rescale = lax.rsqrt(jnp.mean(wide * wide, axis=1, keepdims=True) + EPSILON)
+    nrm[...] = (wide * rescale * student_gain_ref[...]).astype(bf16)
+    pl.semaphore_wait(barrier, len(peers) + T - 1)
+    for k in range(len(peers)):
+        nx(k).start()
+    nb[0, owner_rows(o), :] = nrm[:, columns(o)]
+    sb[owner_rows(o), :] = st[:, columns(o)]
+
+    def iota(shape, axis):
+        return lax.broadcasted_iota(jnp.int32, shape, axis)
+
+    ids = ids_ref[...].astype(f32)
+    ids_column = column_of(ids, iota((share, share), 0) == iota((share, share), 1))
+    vocabulary = id_weight_ref.shape[1]
+    looked = jnp.sum(
+        jnp.where(ids_column == iota((share, vocabulary), 1).astype(f32), id_weight_ref[...], 0.0),
+        axis=1,
+        keepdims=True,
+    )
+    row_of = iota((share, E), 0)
+    counts = column_of(counts_ref[...].astype(f32), lax.rem(row_of, E) == iota((share, E), 1))
+    place = (t * span + lax.div(iota((share, 1), 0), E)).astype(f32)
+    token_weight = jnp.where(place < counts, looked, 0.0).astype(bf16).astype(f32)
+    own_column = owner_ref[...].astype(f32)
+    episode_row, episode_lane = iota((E, 128), 0), lax.rem(iota((E, 128), 1), E)
+    own_lane = jnp.sum(jnp.where(episode_row == episode_lane, own_column, 0.0), axis=0, keepdims=True)
+    rank = jnp.sum(
+        jnp.where((own_column == own_lane) & (episode_row < episode_lane), 1.0, 0.0), axis=0, keepdims=True
+    )
+    target = own_lane * cap + rank
+    ext[o, 0:share, :] = jnp.broadcast_to(token_weight, (share, 128))
+    ext[o, share : share + 8, :] = jnp.broadcast_to(target, (8, 128))
+    for k in range(len(peers)):
+        raw(k).start()
+        extra(k).start()
+
+    loads[1].wait()
+    wide = th[...].astype(f32)
+    scaled[...] = (wide * teacher_gain_ref[...]).astype(bf16)
+    sqs[...] = jnp.broadcast_to(jnp.sum(wide * wide, axis=1, keepdims=True), sqs.shape)
+    for step in range(1, T):
+        squares(step).start()
+    loads[2].wait()
+
+    def teacher_tile(offset, n):
+        tp[:, pl.ds(offset, n)] = jnp.dot(
+            scaled[...], pw[:, pl.ds(offset, n)], preferred_element_type=f32
+        ).astype(bf16)
+
+    over_tiles(DS, teacher_tile)
+    trr[0] = jnp.zeros(trr.shape[1:], bf16)
+    rsr[0] = jnp.zeros(rsr.shape[1:], bf16)
+
+    def teacher_rows(position, d):
+        return pl.ds(pl.multiple_of(at_ring(position) * share + d * t_half, t_half), t_half)
+
+    def teacher_step(k):
+        @pl.when(k > 1)
+        def _():
+            tr(0, k - 1).wait_recv()
+            tr(1, k - 1).wait_recv()
+
+        for d in (0, 1):
+            position = r + T - k if d == 0 else r + k
+            trs[k, part(d, t_half), :] = (
+                tp[teacher_rows(position, d), :].astype(f32) + trr[k - 1, part(d, t_half), :].astype(f32)
+            ).astype(bf16)
+            tr(d, k).start()
+
+    for k in range(len(peers)):
+        nx(k).wait_recv()
+    loads[3].wait()
+    loads[4].wait()
+    loads[5].wait()
+
+    def p1(g):
+        @pl.when(g > 0)
+        def _():
+            ag(0, g).wait_recv()
+            ag(1, g).wait_recv()
+
+        @pl.when(g < T - 1)
+        def _():
+            ag(0, g + 1).start()
+            ag(1, g + 1).start()
+
+        away = pl.ds(pl.multiple_of((1 - c) * half, half), half)
+        here = pl.ds(pl.multiple_of(c * half, half), half)
+        for m, weight in enumerate((gw, uw)):
+
+            def tile(offset, n):
+                lhs = jnp.concatenate([nb[g, away, :], nb[g, here, :]], axis=0)
+                value = jnp.dot(lhs, weight[:, pl.ds(offset, n)], preferred_element_type=f32)
+                d2s[g, m, :, pl.ds(offset, n)] = value[:half].astype(bf16)
+                own_part[m, :, pl.ds(offset, n)] = value[half:]
+
+            over_tiles(H, tile)
+        d2(g).start()
+
+    def p2(g):
+        d2(g).wait_recv()
+        far = pl.ds(pl.multiple_of((1 - x) * quarter, quarter), quarter)
+        near = pl.ds(pl.multiple_of(x * quarter, quarter), quarter)
+        for m in (0, 1):
+            xs[g, m] = (own_part[m, far, :] + d2r[g, m, far, :].astype(f32)).astype(bf16)
+        xch(g).start()
+        for m in (0, 1):
+            own_x[m] = own_part[m, near, :] + d2r[g, m, near, :].astype(f32)
+
+    def p3(g):
+        xch(g).wait_recv()
+        gate = own_x[0] + xr[g, 0].astype(f32)
+        up = own_x[1] + xr[g, 1].astype(f32)
+        act[g, own_act, :] = (gate / (1.0 + jnp.exp(-gate)) * up).astype(bf16)
+        a1(g).start()
+        a2(g).start()
+
+    def p4(g):
+        a1(g).wait_recv()
+        a3(g).start()
+
+    def act_store(g):
+        return pltpu.make_async_copy(act.at[g], act_out.at[g], out_sem.at[0, g])
+
+    def p5(g):
+        a2(g).wait_recv()
+        a3(g).wait_recv()
+        act_store(g).start()
+
+        @pl.when(g > 1)
+        def _():
+            rs(0, g - 1).wait_recv()
+            rs(1, g - 1).wait_recv()
+
+        def tile(offset, n):
+            value = jnp.dot(act[g], dw[:, pl.ds(offset, n)], preferred_element_type=f32)
+
+            @pl.when(g == 0)
+            def _():
+                bp0[:, pl.ds(offset, n)] = value
+
+            @pl.when(g > 0)
+            def _():
+                rss[g, :, pl.ds(offset, n)] = (
+                    value + rsr[jnp.maximum(g - 1, 0), :, pl.ds(offset, n)].astype(f32)
+                ).astype(bf16)
+
+        over_tiles(W, tile)
+
+        @pl.when(g > 0)
+        def _():
+            rs(0, g).start()
+            rs(1, g).start()
+
+    def finish_teacher():
+        tr(0, T - 1).wait_recv()
+        tr(1, T - 1).wait_recv()
+        total = sqs[block_rows(r), :]
+        for step in range(1, T):
+            squares(step).wait_recv()
+            total = total + sqr[step]
+        inverse_ref[...] = lax.rsqrt(total * (1.0 / size["teacher_width"]) + EPSILON)
+        for d in (0, 1):
+            summed = tp[teacher_rows(r, d), :].astype(f32) + trr[T - 1, part(d, t_half), :].astype(f32)
+            pjs[part(d, t_half), :] = (summed * inverse_ref[part(d, t_half), 0:1]).astype(bf16)
+        for k in range(len(peers)):
+            proj(k).start()
+        pj[owner_rows(o), :] = pjs[:, columns(o)]
+
+    def step(i, carry):
+        @pl.when(i < T)
+        def _():
+            p1(i)
+
+        @pl.when(i < T - 1)
+        def _():
+            teacher_step(i + 1)
+
+        @pl.when(i == T - 1)
+        def _():
+            finish_teacher()
+
+        @pl.when(i >= 2)
+        def _():
+            p4(i - 2)
+            p5(i - 2)
+
+        @pl.when((i >= 1) & (i <= T))
+        def _():
+            p3(i - 1)
+
+        @pl.when(i < T)
+        def _():
+            p2(i)
+
+        return carry
+
+    lax.fori_loop(0, T + 2, step, 0)
+
+    for k in range(len(peers)):
+        raw(k).wait_recv()
+        extra(k).wait_recv()
+        proj(k).wait_recv()
+    rs(0, T - 1).wait_recv()
+    rs(1, T - 1).wait_recv()
+    order = [s for pair in zip(range(O // 2), range(O // 2, O)) for s in pair]
+    for s in order:
+        own = slice(s * share, (s + 1) * share)
+        predicted = sb[own, :].astype(f32) + (bp0[own, :] + rsr[T - 1, own, :].astype(f32))
+        predb[own, :] = predicted.astype(bf16)
+        difference = predicted - pj[own, :].astype(f32)
+        ga[0, own, :] = (ext[s, 0:share, 0:1] * difference * size["scale"]).astype(bf16)
+        gg(s, 1).start()
+
+    def grad_store(g):
+        return pltpu.make_async_copy(ga.at[g], grad_out.at[g], out_sem.at[1, g])
+
+    grad_store(0).start()
+
+    lane = iota((1, rows), 1)
+    wanted_target = jnp.zeros((1, rows), f32)
+    for s in range(O):
+        wanted_target = jnp.where(lax.div(lane, share) == s, ext[s, share : share + 1, :], wanted_target)
+    picks = O * out_rows
+    line = iota((picks, rows), 0)
+    place_row = lax.rem(lax.div(line, O * cap), span)
+    source_row = lax.rem(lax.div(line, cap), O)
+    slot = (lax.div(line, out_rows) * cap + lax.rem(line, cap)).astype(f32)
+    lanes = iota((picks, rows), 1)
+    chosen = (
+        (wanted_target == slot)
+        & (lax.div(lanes, share) == source_row)
+        & (lax.div(lax.rem(lanes, share), E) == place_row)
+    )
+    selector = jnp.where(chosen, 1.0, 0.0).astype(bf16)
+
+    def pick_tile(offset, n):
+        sos[:, pl.ds(offset, n)] = jnp.dot(
+            selector, predb[:, pl.ds(offset, n)], preferred_element_type=f32
+        ).astype(bf16)
+
+    over_tiles(W, pick_tile)
+    for k in range(len(peers)):
+        outgoing(k).start()
+    so[:, columns(o)] = sos[pl.ds(pl.multiple_of(o * out_rows, out_rows), out_rows), :]
+
+    def gather_step(g, carry):
+        for s in order:
+            gg(s, g).wait_recv()
+
+            @pl.when(g < T - 1)
+            def _():
+                gg(s, g + 1).start()
+
+        grad_store(g).start()
+        return carry
+
+    lax.fori_loop(1, T, gather_step, 0)
+
+    for k in range(len(peers)):
+        outgoing(k).wait_recv()
+    student_store = pltpu.make_async_copy(so, student_out, out_sem.at[0, T])
+    student_store.start()
+
+    def drain(g, carry):
+        for copy in (d2, xch, a1, a2, a3):
+            copy(g).wait_send()
+        act_store(g).wait()
+        grad_store(g).wait()
+
+        @pl.when(g > 0)
+        def _():
+            squares(g).wait_send()
+            for d in (0, 1):
+                ag(d, g).wait_send()
+                rs(d, g).wait_send()
+                tr(d, g).wait_send()
+            for s in range(O):
+                gg(s, g).wait_send()
+
+        return carry
+
+    lax.fori_loop(0, T, drain, 0)
+    for k in range(len(peers)):
+        nx(k).wait_send()
+        raw(k).wait_send()
+        extra(k).wait_send()
+        proj(k).wait_send()
+        outgoing(k).wait_send()
+    student_store.wait()
+
+
+def fused(
+    teacher_hidden,
+    teacher_gain,
+    project_weight,
+    student_hidden,
+    student_gain,
+    gate_weight,
+    up_weight,
+    down_weight,
+    owner_map,
+    token_ids,
+    token_counts,
+    id_weight,
+):
+    f32, bf16 = jnp.float32, jnp.bfloat16
+    T, O = lax.axis_size("tensor"), lax.axis_size("group") * lax.axis_size("dp")
+    E = token_counts.shape[0]
+    span = EP_LEN // T
+    share = span * E
+    rows = O * share
+    half, quarter = rows // 2, rows // 4
+    cap = max(2, 2 * E // O)
+    local_tokens, F = teacher_hidden.shape
+    DS = student_hidden.shape[1]
+    W, H = gate_weight.shape
+    out_rows = span * O * cap
+    size = dict(
+        T=T,
+        O=O,
+        E=E,
+        span=span,
+        cap=cap,
+        teacher_width=F * T,
+        scale=1.0 / math.sqrt(EP_LEN * E * O),
+    )
+    vmem = pl.BlockSpec(memory_space=pltpu.VMEM)
+    anywhere = pl.BlockSpec(memory_space=pl.ANY)
+    DMA = pltpu.SemaphoreType.DMA
+    scratch = [
+        pltpu.VMEM((local_tokens, F), bf16),
+        pltpu.VMEM((local_tokens, F), bf16),
+        pltpu.VMEM((F, DS), bf16),
+        pltpu.VMEM((local_tokens, DS), bf16),
+        pltpu.VMEM((share, DS), bf16),
+        pltpu.VMEM((share, DS), bf16),
+        pltpu.VMEM((W, H), bf16),
+        pltpu.VMEM((W, H), bf16),
+        pltpu.VMEM((H, W), bf16),
+        pltpu.VMEM((T, rows, W), bf16),
+        pltpu.VMEM((2, half, H), f32),
+        pltpu.VMEM((T, 2, half, H), bf16),
+        pltpu.VMEM((T, 2, half, H), bf16),
+        pltpu.VMEM((2, quarter, H), f32),
+        pltpu.VMEM((T, 2, quarter, H), bf16),
+        pltpu.VMEM((T, 2, quarter, H), bf16),
+        pltpu.VMEM((T, rows, H), bf16),
+        pltpu.VMEM((rows, W), f32),
+        pltpu.VMEM((T, rows, W), bf16),
+        pltpu.VMEM((T, rows, W), bf16),
+        pltpu.VMEM((T, share, DS), bf16),
+        pltpu.VMEM((T, share, DS), bf16),
+        pltpu.VMEM((local_tokens, 128), f32),
+        pltpu.VMEM((T, share, 128), f32),
+        pltpu.VMEM((share, 128), f32),
+        pltpu.VMEM((share, DS), bf16),
+        pltpu.VMEM((rows, W), bf16),
+        pltpu.VMEM((rows, W), bf16),
+        pltpu.VMEM((O, share + 8, 128), f32),
+        pltpu.VMEM((T, rows, W), bf16),
+        pltpu.VMEM((rows, W), bf16),
+        pltpu.VMEM((O * out_rows, W), bf16),
+        pltpu.VMEM((out_rows, DS), bf16),
+        DMA((6,)),
+        *[DMA((3,)) for _ in range(10)],
+        *[DMA((T,)) for _ in range(2)],
+        *[DMA((2, T)) for _ in range(6)],
+        *[DMA((O, T)) for _ in range(2)],
+        *[DMA((T,)) for _ in range(10)],
+        DMA((2, T + 1)),
+    ]
+    grads, acts, out = pl.pallas_call(
+        functools.partial(fused_kernel, size),
+        out_shape=(
+            jax.ShapeDtypeStruct((T, rows, W), bf16),
+            jax.ShapeDtypeStruct((T, rows, H), bf16),
+            jax.ShapeDtypeStruct((out_rows, DS), bf16),
+        ),
+        in_specs=[anywhere, vmem, anywhere, anywhere, vmem, anywhere, anywhere, anywhere, vmem, vmem, vmem, vmem],
+        out_specs=(anywhere, anywhere, anywhere),
+        scratch_shapes=scratch,
+        compiler_params=pltpu.CompilerParams(
+            collective_id=0, has_side_effects=True, vmem_limit_bytes=63 * 1024 * 1024
+        ),
+    )(
+        teacher_hidden,
+        teacher_gain.reshape(1, F),
+        project_weight,
+        student_hidden,
+        student_gain.reshape(1, DS),
+        gate_weight,
+        up_weight,
+        down_weight,
+        owner_map,
+        token_ids.reshape(1, share),
+        token_counts.reshape(1, E),
+        id_weight.reshape(1, -1),
+    )
+    down_grad = jnp.einsum(
+        "rc,rh->ch", grads.reshape(T * rows, W), acts.reshape(T * rows, H), preferred_element_type=f32
+    )
+    return (out.reshape(1, span, O * cap, DS), down_grad)
+
+
+def fits(mesh):
+    return mesh.shape["group"] == 2 and mesh.shape["dp"] == 2 and mesh.shape["tensor"] == 8
+
+
 def solution(mesh):
     in_specs = (
         P(("group", "dp"), "tensor"),
@@ -165,4 +841,5 @@
         P(),
     )
     out_specs = (P(("group", "dp"), "tensor", None, None), P(("group", "dp"), "tensor"))
-    return jax.shard_map(local, mesh=mesh, in_specs=in_specs, out_specs=out_specs, check_vma=False)
+    body = fused if fits(mesh) else general
+    return jax.shard_map(body, mesh=mesh, in_specs=in_specs, out_specs=out_specs, check_vma=False)

time: 379 us -> 129 us (0.34)
  waiting for transfers between devices: 258 us -> 0 us
  Pallas kernels: 0 us -> 111 us
  blocking collectives: 32 us -> 0 us
  matrix products: 29.6 us -> 7.09 us
  other arithmetic: 14.1 us -> 0 us
  between operations: 14.3 us -> 0.66 us
  local copies, waits for them, and re-layouts: 22.6 us -> 10.2 us
  starting transfers between devices: 8.01 us -> 0 us
    reduce_scatter x3 -> x0, waiting for transfers between devices: 148 us -> none  [the longest x1 58.9 us: local(): lax.psum_scatter(branch.astype(jnp.bfloat16), 'tensor', scatter_dimension...]
    pallas_call x0 -> x1, Pallas kernels: none -> 111 us  [fused(): pl.pallas_call(functools.partial(fused_kernel, size), out_shape=(jax.Shap...]
    all_gather x3 -> x0, waiting for transfers between devices: 98.9 us -> none  [the longest x1 47.4 us: local(): gathered = lax.all_gather(normed, 'tensor', axis=0, tiled=True)]
    dot_general x6 -> x1, matrix products: 29.6 us -> 7.09 us  [fused(): jnp.einsum('rc,rh->ch', grads.reshape(T * rows, W), acts.reshape(T * rows...]
    psum x1 -> x0, blocking collectives: 21.4 us -> none  [local(): inverse = lax.rsqrt(lax.psum(squares, 'tensor') / teacher_width + EPSILON)]
    another operation x6 -> x0, local copies, waits for them, and re-layouts: 17.3 us -> none  [the longest x4 17.2 us: local(): jnp.stack([gate_part.astype(jnp.bfloat16).reshape(owners, -1, hidden), up...]
    all_to_all x1 -> x0, blocking collectives: 10.6 us -> none  [exchange(): lax.all_to_all(blocks, OWNER_AXES, split_axis=0, concat_axis=0, tiled=True)]
    all_to_all x2 -> x0, waiting for transfers between devices: 10.5 us -> none  [exchange(): lax.all_to_all(blocks, OWNER_AXES, split_axis=0, concat_axis=0, tiled=True)]
  transfers between devices with their start and end apart: 8 -> 0, of which waited for: 8 -> 0; matrix products, arithmetic and copies ran while one was open for 5% -> 0% of each run, Pallas kernels for 0% -> 0%
where the time goes in v1:
time: 129 us
  Pallas kernels  111 us (86%)
  local copies, waits for them, and re-layouts  10.2 us (8%)
  matrix products  7.09 us (5%)
    pallas_call x1, Pallas kernels, fused(): pl.pallas_call(functools.partial(fused_kernel, size), out_shape=(jax.Shap...  111 us
    unnamed x8, local copies, waits for them, and re-layouts  8.9 us
    dot_general x1, matrix products, fused(): jnp.einsum('rc,rh->ch', grads.reshape(T * rows, W), acts.reshape(T * rows...  7.09 us

profile of v1, /device:TPU:0, one launch (start us, length us, event | category | flops | bytes accessed | tf_op | source)
XLA Modules:
  0.0 129.0 jit_solution(8921026518762114497)
XLA Ops:
  0.6 0.0 copy-start
  0.6 1.5 %copy.16.owner_ref = s32[16,1]{1,0:T(8,128)} copy(s32[16,1]{0,1:T(1,128)} %param.20) | data formatting | bytes 128 | tf_op args[8]
  2.1 1.3 %reshape.25.student_gain_ref = f32[1,3584]{1,0:T(1,128)} reshape(f32[3584]{0:T(1024)} %param.16) | data formatting | bytes 28672 | tf_op jit(solution)/shard_map/reshape | solution.py:809
  3.4 4.1 %copy.14.gate_ref = bf16[896,1184]{1,0:T(8,128)(2,1)} copy(bf16[896,1184]{0,1:T(8,128)(2,1)} %param.17) | data formatting | bytes 4243456 | tf_op args[5]
  7.6 0.0 copy-done
  7.6 2.5 %copy.15.up_ref = bf16[896,1184]{1,0:T(8,128)(2,1)} copy(bf16[896,1184]{0,1:T(8,128)(2,1)S(1)} %copy-done) | data formatting | bytes 4243456 | tf_op args[6]
  10.1 111.0 %shard_map.131 = (bf16[8,128,896]{2,1,0:T(8,128)(2,1)}, bf16[8,128,1184]{2,1,0:T(8,128)(2,1)}, bf16[64,3584]{1,0:T(8,128)(2,1)}) custom-call(bf16[256,1024]{1,0:T(8,128)(2,1)} %teacher_ref.1, f32[1,1024]{1,0:T(1,128)} %bitcast.10, bf16[1024,3584]{1,0:T(8,128)(2,1)} %project_ref.1, bf16[32,3584]{1,0:T(8,128)(2,1)} %student_ref.1, ...), custom_call_target="tpu_custom_call" | custom-call | tf_op jit(solution)/shard_map/pallas_call | solution.py:791
  121.1 0.0 copy-start.1
  121.1 7.1 %convolution_bitcast_fusion = f32[896,1184]{0,1:T(8,128)} fusion(bf16[8,128,896]{2,1,0:T(8,128)(2,1)} %get-tuple-element.6, bf16[8,128,1184]{2,1,0:T(8,128)(2,1)} %get-tuple-element.7), kind=kOutput, calls=%fused_computation | convolution fusion | flops 2172649472 | bytes 8503296 | tf_op jit(solution)/shard_map/rc,rh->ch/dot_general | solution.py:818
  128.2 0.0 copy-done.1
  128.2 0.8 copy.20
Async XLA Ops:
  0.6 6.9 %copy-start = (bf16[896,1184]{0,1:T(8,128)(2,1)S(1)}, bf16[896,1184]{0,1:T(8,128)(2,1)}, u32[]{:S(2)}) copy-start(bf16[896,1184]{0,1:T(8,128)(2,1)} %param.18) | copy-start | bytes 6365188
  121.1 7.1 %copy-start.1 = (bf16[64,3584]{1,0:T(8,128)(2,1)S(1)}, bf16[64,3584]{1,0:T(8,128)(2,1)}, u32[]{:S(2)}) copy-start(bf16[64,3584]{1,0:T(8,128)(2,1)} %get-tuple-element.5) | copy-start | bytes 1376260

commit v2 on v1

--- a/solution.py
+++ b/solution.py
@@ -207,7 +207,7 @@
     xs,
     xr,
     act,
-    bp0,
+    bp,
     rss,
     rsr,
     trs,
@@ -261,7 +261,7 @@
     rows = O * share
     half, quarter = rows // 2, rows // 4
     W = nb.shape[2]
-    H = gw.shape[1]
+    H = gw.shape[0]
     DS = st.shape[1]
     t_half = share // 2
     f32, bf16 = jnp.float32, jnp.bfloat16
@@ -377,9 +377,9 @@
             nb.at[g - 1, part(d, half), :], nb.at[g, part(d, half), :], ag_s.at[d, g], ag_r.at[d, g], to(d)
         )
 
-    def rs(d, g):
+    def rs(s, g):
         return remote(
-            rss.at[g, part(d, half), :], rsr.at[g, part(d, half), :], rs_s.at[d, g], rs_r.at[d, g], to(d)
+            rss.at[g, part(s, share), :], rsr.at[g, part(s, share), :], rs_s.at[s, g], rs_r.at[s, g], to(s * 2 // O)
         )
 
     def tr(d, k):
@@ -387,17 +387,32 @@
             trs.at[k, part(d, t_half), :], trr.at[k, part(d, t_half), :], tr_s.at[d, k], tr_r.at[d, k], to(d)
         )
 
-    def gg(s, g):
-        d = s * 2 // O
+    def slot_of(d, s, k):
+        return k if (d == 0) == (s < O // 2) else lax.rem(T - k, T)
+
+    def gg(d, s, k):
         return remote(
-            ga.at[g - 1, part(s, share), :], ga.at[g, part(s, share), :], gg_s.at[s, g], gg_r.at[s, g], to(d)
-        )
-
-    def d2(g):
-        return remote(d2s.at[g], d2r.at[g], d2_s.at[g], d2_r.at[g], core_peer)
-
-    def xch(g):
-        return remote(xs.at[g], xr.at[g], x_s.at[g], x_r.at[g], other_chip)
+            ga.at[slot_of(d, s, k - 1), part(s, share), :],
+            ga.at[slot_of(d, s, k), part(s, share), :],
+            gg_s.at[d * O + s, k],
+            gg_r.at[d * O + s, k],
+            to(d),
+        )
+
+    def gg_order():
+        ahead, behind = list(range(O // 2)), list(range(O // 2, O))
+        return [pair for a, b in zip(ahead + behind, behind + ahead) for pair in ((0, a), (1, b))]
+
+    def goes_on(d, s):
+        return (d == 0) == (s < O // 2)
+
+    order = [s for pair in zip(range(O // 2), range(O // 2, O)) for s in pair]
+
+    def d2(g, m):
+        return remote(d2s.at[g, m], d2r.at[g, m], d2_s.at[m, g], d2_r.at[m, g], core_peer)
+
+    def xch(g, m):
+        return remote(xs.at[g, m], xr.at[g, m], x_s.at[m, g], x_r.at[m, g], other_chip)
 
     def act_rows(core, chip):
         return pl.ds(pl.multiple_of((core * 2 + chip) * quarter, quarter), quarter)
@@ -417,7 +432,9 @@
     loads[0].wait()
     wide = st[...].astype(f32)
     rescale = lax.rsqrt(jnp.mean(wide * wide, axis=1, keepdims=True) + EPSILON)
-    nrm[...] = (wide * rescale * student_gain_ref[...]).astype(bf16)
+    for j in range(DS // 128):
+        lanes = slice(j * 128, (j + 1) * 128)
+        nrm[:, lanes] = (wide[:, lanes] * rescale * student_gain_ref[j : j + 1, :]).astype(bf16)
     pl.semaphore_wait(barrier, len(peers) + T - 1)
     for k in range(len(peers)):
         nx(k).start()
@@ -439,7 +456,7 @@
     counts = column_of(counts_ref[...].astype(f32), lax.rem(row_of, E) == iota((share, E), 1))
     place = (t * span + lax.div(iota((share, 1), 0), E)).astype(f32)
     token_weight = jnp.where(place < counts, looked, 0.0).astype(bf16).astype(f32)
-    own_column = owner_ref[...].astype(f32)
+    own_column = column_of(owner_ref[...].astype(f32), iota((E, E), 0) == iota((E, E), 1))
     episode_row, episode_lane = iota((E, 128), 0), lax.rem(iota((E, 128), 1), E)
     own_lane = jnp.sum(jnp.where(episode_row == episode_lane, own_column, 0.0), axis=0, keepdims=True)
     rank = jnp.sum(
@@ -465,7 +482,34 @@
             scaled[...], pw[:, pl.ds(offset, n)], preferred_element_type=f32
         ).astype(bf16)
 
-    over_tiles(DS, teacher_tile)
+    def forward(k):
+        @pl.when(k > 0)
+        def _():
+            ag(0, k).wait_recv()
+            ag(1, k).wait_recv()
+
+        @pl.when(k < T - 1)
+        def _():
+            ag(0, k + 1).start()
+            ag(1, k + 1).start()
+
+    whole = DS // TILE
+    early = whole * 2 // 3
+
+    def teacher_loop(index, carry):
+        teacher_tile(pl.multiple_of(index * TILE, TILE), TILE)
+        return carry
+
+    lax.fori_loop(0, early, teacher_loop, 0)
+    for k in range(len(peers)):
+        nx(k).wait_recv()
+    forward(0)
+
+    def teacher_rest():
+        lax.fori_loop(early, whole, teacher_loop, 0)
+        if DS > whole * TILE:
+            teacher_tile(whole * TILE, DS - whole * TILE)
+
     trr[0] = jnp.zeros(trr.shape[1:], bf16)
     rsr[0] = jnp.zeros(rsr.shape[1:], bf16)
 
@@ -485,50 +529,41 @@
             ).astype(bf16)
             tr(d, k).start()
 
-    for k in range(len(peers)):
-        nx(k).wait_recv()
     loads[3].wait()
     loads[4].wait()
     loads[5].wait()
 
     def p1(g):
-        @pl.when(g > 0)
-        def _():
-            ag(0, g).wait_recv()
-            ag(1, g).wait_recv()
-
-        @pl.when(g < T - 1)
-        def _():
-            ag(0, g + 1).start()
-            ag(1, g + 1).start()
-
         away = pl.ds(pl.multiple_of((1 - c) * half, half), half)
         here = pl.ds(pl.multiple_of(c * half, half), half)
         for m, weight in enumerate((gw, uw)):
 
             def tile(offset, n):
                 lhs = jnp.concatenate([nb[g, away, :], nb[g, here, :]], axis=0)
-                value = jnp.dot(lhs, weight[:, pl.ds(offset, n)], preferred_element_type=f32)
+                value = lax.dot_general(
+                    lhs, weight[pl.ds(offset, n), :], (((1,), (1,)), ((), ())), preferred_element_type=f32
+                )
                 d2s[g, m, :, pl.ds(offset, n)] = value[:half].astype(bf16)
                 own_part[m, :, pl.ds(offset, n)] = value[half:]
 
             over_tiles(H, tile)
-        d2(g).start()
+            d2(g, m).start()
 
     def p2(g):
-        d2(g).wait_recv()
         far = pl.ds(pl.multiple_of((1 - x) * quarter, quarter), quarter)
         near = pl.ds(pl.multiple_of(x * quarter, quarter), quarter)
         for m in (0, 1):
+            d2(g, m).wait_recv()
             xs[g, m] = (own_part[m, far, :] + d2r[g, m, far, :].astype(f32)).astype(bf16)
-        xch(g).start()
+            xch(g, m).start()
         for m in (0, 1):
-            own_x[m] = own_part[m, near, :] + d2r[g, m, near, :].astype(f32)
+            own_x[g, m] = own_part[m, near, :] + d2r[g, m, near, :].astype(f32)
 
     def p3(g):
-        xch(g).wait_recv()
-        gate = own_x[0] + xr[g, 0].astype(f32)
-        up = own_x[1] + xr[g, 1].astype(f32)
+        xch(g, 0).wait_recv()
+        xch(g, 1).wait_recv()
+        gate = own_x[g, 0] + xr[g, 0].astype(f32)
+        up = own_x[g, 1] + xr[g, 1].astype(f32)
         act[g, own_act, :] = (gate / (1.0 + jnp.exp(-gate)) * up).astype(bf16)
         a1(g).start()
         a2(g).start()
@@ -545,30 +580,24 @@
         a3(g).wait_recv()
         act_store(g).start()
 
-        @pl.when(g > 1)
-        def _():
-            rs(0, g - 1).wait_recv()
-            rs(1, g - 1).wait_recv()
+        kept = jnp.minimum(g, 1)
 
         def tile(offset, n):
-            value = jnp.dot(act[g], dw[:, pl.ds(offset, n)], preferred_element_type=f32)
-
-            @pl.when(g == 0)
-            def _():
-                bp0[:, pl.ds(offset, n)] = value
-
-            @pl.when(g > 0)
-            def _():
-                rss[g, :, pl.ds(offset, n)] = (
-                    value + rsr[jnp.maximum(g - 1, 0), :, pl.ds(offset, n)].astype(f32)
-                ).astype(bf16)
+            bp[kept, :, pl.ds(offset, n)] = jnp.dot(act[g], dw[:, pl.ds(offset, n)], preferred_element_type=f32)
 
         over_tiles(W, tile)
 
         @pl.when(g > 0)
         def _():
-            rs(0, g).start()
-            rs(1, g).start()
+            for s in order:
+
+                @pl.when(g > 1)
+                def _():
+                    rs(s, g - 1).wait_recv()
+
+                own = part(s, share)
+                rss[g, own, :] = (bp[1, own, :] + rsr[g - 1, own, :].astype(f32)).astype(bf16)
+                rs(s, g).start()
 
     def finish_teacher():
         tr(0, T - 1).wait_recv()
@@ -585,50 +614,66 @@
             proj(k).start()
         pj[owner_rows(o), :] = pjs[:, columns(o)]
 
+    first = T // 2
+
     def step(i, carry):
         @pl.when(i < T)
         def _():
             p1(i)
 
-        @pl.when(i < T - 1)
+        @pl.when(i + 1 < T)
+        def _():
+            forward(i + 1)
+
+        @pl.when((i >= 3) & (i < T + 3))
+        def _():
+            p4(i - 3)
+
+        @pl.when(i == 0)
+        def _():
+            teacher_rest()
+
+        @pl.when(i < first)
         def _():
             teacher_step(i + 1)
 
-        @pl.when(i == T - 1)
+        @pl.when((i >= T - 1) & (i < T + T - 2 - first))
+        def _():
+            teacher_step(i - (T - 2 - first))
+
+        @pl.when(i == T + T - 2 - first)
         def _():
             finish_teacher()
 
-        @pl.when(i >= 2)
-        def _():
-            p4(i - 2)
-            p5(i - 2)
-
-        @pl.when((i >= 1) & (i <= T))
-        def _():
-            p3(i - 1)
+        @pl.when((i >= 2) & (i < T + 2))
+        def _():
+            p3(i - 2)
 
         @pl.when(i < T)
         def _():
             p2(i)
 
+        @pl.when(i >= 3)
+        def _():
+            p5(i - 3)
+
         return carry
 
-    lax.fori_loop(0, T + 2, step, 0)
+    lax.fori_loop(0, T + 3, step, 0)
 
     for k in range(len(peers)):
         raw(k).wait_recv()
         extra(k).wait_recv()
         proj(k).wait_recv()
-    rs(0, T - 1).wait_recv()
-    rs(1, T - 1).wait_recv()
-    order = [s for pair in zip(range(O // 2), range(O // 2, O)) for s in pair]
     for s in order:
+        rs(s, T - 1).wait_recv()
         own = slice(s * share, (s + 1) * share)
-        predicted = sb[own, :].astype(f32) + (bp0[own, :] + rsr[T - 1, own, :].astype(f32))
+        predicted = sb[own, :].astype(f32) + (bp[0, own, :] + rsr[T - 1, own, :].astype(f32))
         predb[own, :] = predicted.astype(bf16)
         difference = predicted - pj[own, :].astype(f32)
         ga[0, own, :] = (ext[s, 0:share, 0:1] * difference * size["scale"]).astype(bf16)
-        gg(s, 1).start()
+        for d in (0, 1):
+            gg(d, s, 1).start()
 
     def grad_store(g):
         return pltpu.make_async_copy(ga.at[g], grad_out.at[g], out_sem.at[1, g])
@@ -662,18 +707,35 @@
         outgoing(k).start()
     so[:, columns(o)] = sos[pl.ds(pl.multiple_of(o * out_rows, out_rows), out_rows), :]
 
-    def gather_step(g, carry):
-        for s in order:
-            gg(s, g).wait_recv()
-
-            @pl.when(g < T - 1)
-            def _():
-                gg(s, g + 1).start()
-
-        grad_store(g).start()
+    far_hop = T // 2
+
+    def gather_step(k, carry):
+        for d, s in gg_order():
+            if goes_on(d, s):
+                gg(d, s, k).wait_recv()
+
+                @pl.when(k < far_hop)
+                def _():
+                    gg(d, s, k + 1).start()
+            else:
+
+                @pl.when(k < far_hop)
+                def _():
+                    gg(d, s, k).wait_recv()
+
+                @pl.when(k < far_hop - 1)
+                def _():
+                    gg(d, s, k + 1).start()
+
+        grad_store(k).start()
+
+        @pl.when(k < far_hop)
+        def _():
+            grad_store(T - k).start()
+
         return carry
 
-    lax.fori_loop(1, T, gather_step, 0)
+    lax.fori_loop(1, far_hop + 1, gather_step, 0)
 
     for k in range(len(peers)):
         outgoing(k).wait_recv()
@@ -681,8 +743,11 @@
     student_store.start()
 
     def drain(g, carry):
-        for copy in (d2, xch, a1, a2, a3):
+        for copy in (a1, a2, a3):
             copy(g).wait_send()
+        for m in (0, 1):
+            d2(g, m).wait_send()
+            xch(g, m).wait_send()
         act_store(g).wait()
         grad_store(g).wait()
 
@@ -691,10 +756,20 @@
             squares(g).wait_send()
             for d in (0, 1):
                 ag(d, g).wait_send()
-                rs(d, g).wait_send()
                 tr(d, g).wait_send()
             for s in range(O):
-                gg(s, g).wait_send()
+                rs(s, g).wait_send()
+
+        @pl.when((g > 0) & (g <= far_hop))
+        def _():
+            for d, s in gg_order():
+                if goes_on(d, s):
+                    gg(d, s, g).wait_send()
+                else:
+
+                    @pl.when(g < far_hop)
+                    def _():
+                        gg(d, s, g).wait_send()
 
         return carry
 
@@ -753,18 +828,18 @@
         pltpu.VMEM((local_tokens, DS), bf16),
         pltpu.VMEM((share, DS), bf16),
         pltpu.VMEM((share, DS), bf16),
-        pltpu.VMEM((W, H), bf16),
-        pltpu.VMEM((W, H), bf16),
+        pltpu.VMEM((H, W), bf16),
+        pltpu.VMEM((H, W), bf16),
         pltpu.VMEM((H, W), bf16),
         pltpu.VMEM((T, rows, W), bf16),
         pltpu.VMEM((2, half, H), f32),
         pltpu.VMEM((T, 2, half, H), bf16),
         pltpu.VMEM((T, 2, half, H), bf16),
-        pltpu.VMEM((2, quarter, H), f32),
+        pltpu.VMEM((T, 2, quarter, H), f32),
         pltpu.VMEM((T, 2, quarter, H), bf16),
         pltpu.VMEM((T, 2, quarter, H), bf16),
         pltpu.VMEM((T, rows, H), bf16),
-        pltpu.VMEM((rows, W), f32),
+        pltpu.VMEM((2, rows, W), f32),
         pltpu.VMEM((T, rows, W), bf16),
         pltpu.VMEM((T, rows, W), bf16),
         pltpu.VMEM((T, share, DS), bf16),
@@ -783,9 +858,11 @@
         DMA((6,)),
         *[DMA((3,)) for _ in range(10)],
         *[DMA((T,)) for _ in range(2)],
-        *[DMA((2, T)) for _ in range(6)],
+        *[DMA((2, T)) for _ in range(4)],
         *[DMA((O, T)) for _ in range(2)],
-        *[DMA((T,)) for _ in range(10)],
+        *[DMA((2 * O, T // 2 + 1)) for _ in range(2)],
+        *[DMA((2, T)) for _ in range(4)],
+        *[DMA((T,)) for _ in range(6)],
         DMA((2, T + 1)),
     ]
     grads, acts, out = pl.pallas_call(
@@ -806,11 +883,11 @@
         teacher_gain.reshape(1, F),
         project_weight,
         student_hidden,
-        student_gain.reshape(1, DS),
-        gate_weight,
-        up_weight,
+        student_gain.reshape(DS // 128, 128),
+        gate_weight.T,
+        up_weight.T,
         down_weight,
-        owner_map,
+        owner_map.reshape(1, E),
         token_ids.reshape(1, share),
         token_counts.reshape(1, E),
         id_weight.reshape(1, -1),

time: 129 us -> 105 us (0.81)
  Pallas kernels: 111 us -> 96 us
  local copies, waits for them, and re-layouts: 10.2 us -> 0.77 us
    pallas_call x1, Pallas kernels: 111 us -> 96 us  [fused(): pl.pallas_call(functools.partial(fused_kernel, size), out_shape=(jax.Shap...]
    unnamed x8 -> x3, local copies, waits for them, and re-layouts: 8.9 us -> 0.77 us
    reshape x1 -> x0, local copies, waits for them, and re-layouts: 1.33 us -> none  [fused(): student_gain.reshape(1, DS)]
where the time goes in v2:
time: 105 us
  Pallas kernels  96 us (91%)
  matrix products  7.1 us (7%)
    pallas_call x1, Pallas kernels, fused(): pl.pallas_call(functools.partial(fused_kernel, size), out_shape=(jax.Shap...  96 us
    dot_general x1, matrix products, fused(): jnp.einsum('rc,rh->ch', grads.reshape(T * rows, W), acts.reshape(T * rows...  7.1 us

profile of v2, /device:TPU:0, one launch (start us, length us, event | category | flops | bytes accessed | tf_op | source)
XLA Modules:
  0.0 104.5 jit_solution(8973373074943939918)
XLA Ops:
  0.6 96.0 %shard_map.131 = (bf16[8,128,896]{2,1,0:T(8,128)(2,1)}, bf16[8,128,1184]{2,1,0:T(8,128)(2,1)}, bf16[64,3584]{1,0:T(8,128)(2,1)}) custom-call(bf16[256,1024]{1,0:T(8,128)(2,1)} %teacher_ref.1, f32[1,1024]{1,0:T(1,128)} %bitcast.17, bf16[1024,3584]{1,0:T(8,128)(2,1)} %project_ref.1, bf16[32,3584]{1,0:T(8,128)(2,1)} %student_ref.1, f32[28,128]{1,0:T(8,128)} %bitcast.16, ...), custom_call_target="tpu_custom_call" | custom-call | tf_op jit(solution)/shard_map/pallas_call | solution.py:868
  96.7 0.0 copy-start
  96.7 7.1 %convolution_bitcast_fusion = f32[896,1184]{0,1:T(8,128)} fusion(bf16[8,128,896]{2,1,0:T(8,128)(2,1)} %get-tuple-element.6, bf16[8,128,1184]{2,1,0:T(8,128)(2,1)} %get-tuple-element.7), kind=kOutput, calls=%fused_computation | convolution fusion | flops 2172649472 | bytes 8503296 | tf_op jit(solution)/shard_map/rc,rh->ch/dot_general | solution.py:895
  103.8 0.0 copy-done
  103.8 0.8 copy.17
Async XLA Ops:
  96.7 7.1 %copy-start = (bf16[64,3584]{1,0:T(8,128)(2,1)S(1)}, bf16[64,3584]{1,0:T(8,128)(2,1)}, u32[]{:S(2)}) copy-start(bf16[64,3584]{1,0:T(8,128)(2,1)} %get-tuple-element.5) | copy-start | bytes 1376260

commit v3 on v2

--- a/solution.py
+++ b/solution.py
@@ -153,7 +153,8 @@
 
 
 MESH = pl.DeviceIdType.MESH
-TILE = 256
+TILE = 1024
+TAIL = 256
 
 
 def over_tiles(width, body):
@@ -190,6 +191,7 @@
     grad_out,
     act_out,
     student_out,
+    sum_out,
     th,
     scaled,
     pw,
@@ -220,6 +222,8 @@
     sb,
     ext,
     ga,
+    act_t,
+    acc,
     predb,
     sos,
     so,
@@ -572,13 +576,12 @@
         a1(g).wait_recv()
         a3(g).start()
 
-    def act_store(g):
-        return pltpu.make_async_copy(act.at[g], act_out.at[g], out_sem.at[0, g])
+    far_hop = T // 2
+    act_store = pltpu.make_async_copy(act_t.at[far_hop], act_out, out_sem.at[0])
 
     def p5(g):
         a2(g).wait_recv()
         a3(g).wait_recv()
-        act_store(g).start()
 
         kept = jnp.minimum(g, 1)
 
@@ -598,6 +601,12 @@
                 own = part(s, share)
                 rss[g, own, :] = (bp[1, own, :] + rsr[g - 1, own, :].astype(f32)).astype(bf16)
                 rs(s, g).start()
+
+        act_t[g] = act[g].T
+
+        @pl.when(g == far_hop)
+        def _():
+            act_store.start()
 
     def finish_teacher():
         tr(0, T - 1).wait_recv()
@@ -629,29 +638,29 @@
         def _():
             p4(i - 3)
 
-        @pl.when(i == 0)
-        def _():
-            teacher_rest()
+        @pl.when((i >= T - 1) & (i < T + T - 2 - first))
+        def _():
+            teacher_step(i - (T - 2 - first))
+
+        @pl.when(i == T + T - 2 - first)
+        def _():
+            finish_teacher()
+
+        @pl.when((i >= 2) & (i < T + 2))
+        def _():
+            p3(i - 2)
+
+        @pl.when(i < T)
+        def _():
+            p2(i)
 
         @pl.when(i < first)
         def _():
+            @pl.when(i == 0)
+            def _():
+                teacher_rest()
+
             teacher_step(i + 1)
-
-        @pl.when((i >= T - 1) & (i < T + T - 2 - first))
-        def _():
-            teacher_step(i - (T - 2 - first))
-
-        @pl.when(i == T + T - 2 - first)
-        def _():
-            finish_teacher()
-
-        @pl.when((i >= 2) & (i < T + 2))
-        def _():
-            p3(i - 2)
-
-        @pl.when(i < T)
-        def _():
-            p2(i)
 
         @pl.when(i >= 3)
         def _():
@@ -675,10 +684,12 @@
         for d in (0, 1):
             gg(d, s, 1).start()
 
-    def grad_store(g):
-        return pltpu.make_async_copy(ga.at[g], grad_out.at[g], out_sem.at[1, g])
-
-    grad_store(0).start()
+    grad_store = pltpu.make_async_copy(ga.at[far_hop], grad_out, out_sem.at[1])
+    pieces = [slice(j, min(j + TAIL, W)) for j in range(0, W, TAIL)]
+    sum_stores = [
+        pltpu.make_async_copy(acc.at[:, lanes], sum_out.at[:, lanes], out_sem.at[3 + j])
+        for j, lanes in enumerate(pieces)
+    ]
 
     lane = iota((1, rows), 1)
     wanted_target = jnp.zeros((1, rows), f32)
@@ -707,10 +718,21 @@
         outgoing(k).start()
     so[:, columns(o)] = sos[pl.ds(pl.multiple_of(o * out_rows, out_rows), out_rows), :]
 
-    far_hop = T // 2
+    def product(k, lanes):
+        @pl.when(k == 0)
+        def _():
+            acc[:, lanes] = jnp.dot(act_t[0], ga[0, :, lanes], preferred_element_type=f32)
+
+        @pl.when(k > 0)
+        def _():
+            near, back = jnp.maximum(k, 1), T - jnp.maximum(k, 1)
+            lhs = jnp.concatenate([act_t[near], act_t[back]], axis=1)
+            rhs = jnp.concatenate([ga[near, :, lanes], ga[back, :, lanes]], axis=0)
+            acc[:, lanes] += jnp.dot(lhs, rhs, preferred_element_type=f32)
 
     def gather_step(k, carry):
-        for d, s in gg_order():
+        steps = gg_order()
+        for index, (d, s) in enumerate(steps):
             if goes_on(d, s):
                 gg(d, s, k).wait_recv()
 
@@ -727,19 +749,21 @@
                 def _():
                     gg(d, s, k + 1).start()
 
-        grad_store(k).start()
-
-        @pl.when(k < far_hop)
-        def _():
-            grad_store(T - k).start()
+            for j in range(index * len(pieces) // len(steps), (index + 1) * len(pieces) // len(steps)):
+                product(k - 1, pieces[j])
+
+                @pl.when(k == far_hop)
+                def _():
+                    sum_stores[j].start()
 
         return carry
 
     lax.fori_loop(1, far_hop + 1, gather_step, 0)
+    grad_store.start()
 
     for k in range(len(peers)):
         outgoing(k).wait_recv()
-    student_store = pltpu.make_async_copy(so, student_out, out_sem.at[0, T])
+    student_store = pltpu.make_async_copy(so, student_out, out_sem.at[2])
     student_store.start()
 
     def drain(g, carry):
@@ -748,8 +772,6 @@
         for m in (0, 1):
             d2(g, m).wait_send()
             xch(g, m).wait_send()
-        act_store(g).wait()
-        grad_store(g).wait()
 
         @pl.when(g > 0)
         def _():
@@ -780,7 +802,36 @@
         extra(k).wait_send()
         proj(k).wait_send()
         outgoing(k).wait_send()
-    student_store.wait()
+    for copy in (act_store, grad_store, student_store, *sum_stores):
+        copy.wait()
+
+
+def last_terms(
+    sum_ref, act_ref, grad_ref, student_ref, out_ref, student_out, total, act, grad, student, small_sem, in_sem, out_sem
+):
+    height = total.shape[0]
+    blocks = [pl.ds(j, min(TAIL, height - j)) for j in range(0, height, TAIL)]
+    small = [
+        pltpu.make_async_copy(act_ref, act, small_sem.at[0]),
+        pltpu.make_async_copy(grad_ref, grad, small_sem.at[1]),
+    ]
+    student_load = pltpu.make_async_copy(student_ref, student, small_sem.at[2])
+    student_store = pltpu.make_async_copy(student, student_out, small_sem.at[3])
+    loads = [pltpu.make_async_copy(sum_ref.at[b, :], total.at[b, :], in_sem.at[j]) for j, b in enumerate(blocks)]
+    stores = [pltpu.make_async_copy(total.at[b, :], out_ref.at[b, :], out_sem.at[j]) for j, b in enumerate(blocks)]
+    for copy in (*small, *loads, student_load):
+        copy.start()
+    for copy in small:
+        copy.wait()
+    for b, load, store in zip(blocks, loads, stores):
+        term = jnp.dot(act[b, :], grad[...], preferred_element_type=jnp.float32)
+        load.wait()
+        total[b, :] += term
+        store.start()
+    student_load.wait()
+    student_store.start()
+    for copy in (*stores, student_store):
+        copy.wait()
 
 
 def fused(
@@ -852,6 +903,8 @@
         pltpu.VMEM((rows, W), bf16),
         pltpu.VMEM((O, share + 8, 128), f32),
         pltpu.VMEM((T, rows, W), bf16),
+        pltpu.VMEM((T, H, rows), bf16),
+        pltpu.VMEM((H, W), f32),
         pltpu.VMEM((rows, W), bf16),
         pltpu.VMEM((O * out_rows, W), bf16),
         pltpu.VMEM((out_rows, DS), bf16),
@@ -863,17 +916,18 @@
         *[DMA((2 * O, T // 2 + 1)) for _ in range(2)],
         *[DMA((2, T)) for _ in range(4)],
         *[DMA((T,)) for _ in range(6)],
-        DMA((2, T + 1)),
+        DMA((3 + pl.cdiv(W, TAIL),)),
     ]
-    grads, acts, out = pl.pallas_call(
+    grads, acts, out, summed = pl.pallas_call(
         functools.partial(fused_kernel, size),
         out_shape=(
-            jax.ShapeDtypeStruct((T, rows, W), bf16),
-            jax.ShapeDtypeStruct((T, rows, H), bf16),
+            jax.ShapeDtypeStruct((rows, W), bf16),
+            jax.ShapeDtypeStruct((H, rows), bf16),
             jax.ShapeDtypeStruct((out_rows, DS), bf16),
+            jax.ShapeDtypeStruct((H, W), f32),
         ),
         in_specs=[anywhere, vmem, anywhere, anywhere, vmem, anywhere, anywhere, anywhere, vmem, vmem, vmem, vmem],
-        out_specs=(anywhere, anywhere, anywhere),
+        out_specs=(anywhere, anywhere, anywhere, anywhere),
         scratch_shapes=scratch,
         compiler_params=pltpu.CompilerParams(
             collective_id=0, has_side_effects=True, vmem_limit_bytes=63 * 1024 * 1024
@@ -892,10 +946,24 @@
         token_counts.reshape(1, E),
         id_weight.reshape(1, -1),
     )
-    down_grad = jnp.einsum(
-        "rc,rh->ch", grads.reshape(T * rows, W), acts.reshape(T * rows, H), preferred_element_type=f32
-    )
-    return (out.reshape(1, span, O * cap, DS), down_grad)
+    blocks = pl.cdiv(H, TAIL)
+    down_grad, out = pl.pallas_call(
+        last_terms,
+        out_shape=(jax.ShapeDtypeStruct((H, W), f32), jax.ShapeDtypeStruct((out_rows, DS), bf16)),
+        in_specs=[anywhere] * 4,
+        out_specs=(anywhere, anywhere),
+        scratch_shapes=[
+            pltpu.VMEM((H, W), f32),
+            pltpu.VMEM((H, rows), bf16),
+            pltpu.VMEM((rows, W), bf16),
+            pltpu.VMEM((out_rows, DS), bf16),
+            DMA((4,)),
+            DMA((blocks,)),
+            DMA((blocks,)),
+        ],
+        compiler_params=pltpu.CompilerParams(vmem_limit_bytes=63 * 1024 * 1024),
+    )(summed, acts, grads, out)
+    return (out.reshape(1, span, O * cap, DS), down_grad.T)
 
 
 def fits(mesh):

time: 105 us -> 99.6 us (0.949)
  matrix products: 7.1 us -> 0 us
  Pallas kernels: 96 us -> 98.7 us
    dot_general x1 -> x0, matrix products: 7.1 us -> none  [fused(): jnp.einsum('rc,rh->ch', grads.reshape(T * rows, W), acts.reshape(T * rows...]
    pallas_call x0 -> x1, Pallas kernels: none -> 4.75 us  [fused(): pl.pallas_call(last_terms, out_shape=(jax.ShapeDtypeStruct((H, W), f32),...]
    pallas_call x1, Pallas kernels: 96 us -> 94 us  [fused(): pl.pallas_call(functools.partial(fused_kernel, size), out_shape=(jax.Shap...]
where the time goes in v3:
time: 99.6 us; the launch traced here: 99.4 us
  Pallas kernels  98.7 us (99%)
    pallas_call x1, Pallas kernels, fused(): pl.pallas_call(functools.partial(fused_kernel, size), out_shape=(jax.Shap...  94 us
    pallas_call x1, Pallas kernels, fused(): pl.pallas_call(last_terms, out_shape=(jax.ShapeDtypeStruct((H, W), f32),...  4.75 us

profile of v3, /device:TPU:0, one launch (start us, length us, event | category | flops | bytes accessed | tf_op | source)
XLA Modules:
  0.0 99.4 jit_solution(2778951551624825802)
XLA Ops:
  0.6 94.0 %shard_map.131 = (bf16[128,896]{1,0:T(8,128)(2,1)}, bf16[1184,128]{1,0:T(8,128)(2,1)}, bf16[64,3584]{1,0:T(8,128)(2,1)}, f32[1184,896]{1,0:T(8,128)}) custom-call(bf16[256,1024]{1,0:T(8,128)(2,1)} %teacher_ref.1, f32[1,1024]{1,0:T(1,128)} %bitcast.13, bf16[1024,3584]{1,0:T(8,128)(2,1)} %project_ref.1, bf16[32,3584]{1,0:T(8,128)(2,1)} %student_ref.1, ...), custom_call_target="tpu_custom_call" | custom-call | tf_op jit(solution)/shard_map/pallas_call | solution.py:921
  94.6 4.8 %shard_map.132 = (f32[1184,896]{1,0:T(8,128)}, bf16[64,3584]{1,0:T(8,128)(2,1)}) custom-call(f32[1184,896]{1,0:T(8,128)} %get-tuple-element.8.sum_ref, bf16[1184,128]{1,0:T(8,128)(2,1)} %get-tuple-element.9.act_ref, bf16[128,896]{1,0:T(8,128)(2,1)} %get-tuple-element.10.grad_ref, bf16[64,3584]{1,0:T(8,128)(2,1)} %get-tuple-element.11.student_ref), custom_call_target="tpu_custom_call" | custom-call | tf_op jit(solution)/shard_map/pallas_call | solution.py:950

commit v4 on v3

--- a/solution.py
+++ b/solution.py
@@ -177,17 +177,17 @@
 def fused_kernel(
     size,
     teacher_ref,
-    teacher_gain_ref,
+    teacher_gain_in,
     project_ref,
     student_ref,
-    student_gain_ref,
+    student_gain_in,
     gate_ref,
     up_ref,
     down_ref,
-    owner_ref,
-    ids_ref,
-    counts_ref,
-    id_weight_ref,
+    owner_in,
+    ids_in,
+    counts_in,
+    id_weight_in,
     grad_out,
     act_out,
     student_out,
@@ -227,6 +227,12 @@
     predb,
     sos,
     so,
+    student_gain_ref,
+    owner_ref,
+    ids_ref,
+    counts_ref,
+    id_weight_ref,
+    teacher_gain_ref,
     load_sem,
     nx_s,
     nx_r,
@@ -301,7 +307,20 @@
             [(student_ref, st), (teacher_ref, th), (project_ref, pw), (gate_ref, gw), (up_ref, uw), (down_ref, dw)]
         )
     ]
-    for load in loads:
+    small = [
+        pltpu.make_async_copy(src, dst, load_sem.at[len(loads) + index])
+        for index, (src, dst) in enumerate(
+            [
+                (student_gain_in, student_gain_ref),
+                (owner_in, owner_ref),
+                (ids_in, ids_ref),
+                (counts_in, counts_ref),
+                (id_weight_in, id_weight_ref),
+                (teacher_gain_in, teacher_gain_ref),
+            ]
+        )
+    ]
+    for load in (loads[0], *small, *loads[1:]):
         load.start()
 
     barrier = pltpu.get_barrier_semaphore()
@@ -404,8 +423,7 @@
         )
 
     def gg_order():
-        ahead, behind = list(range(O // 2)), list(range(O // 2, O))
-        return [pair for a, b in zip(ahead + behind, behind + ahead) for pair in ((0, a), (1, b))]
+        return [(d, s) for s in order for d in (0, 1)]
 
     def goes_on(d, s):
         return (d == 0) == (s < O // 2)
@@ -434,6 +452,7 @@
         return remote(act.at[g, far_act, :], act.at[g, far_act, :], a3_s.at[g], a3_r.at[g], core_peer)
 
     loads[0].wait()
+    small[0].wait()
     wide = st[...].astype(f32)
     rescale = lax.rsqrt(jnp.mean(wide * wide, axis=1, keepdims=True) + EPSILON)
     for j in range(DS // 128):
@@ -448,6 +467,8 @@
     def iota(shape, axis):
         return lax.broadcasted_iota(jnp.int32, shape, axis)
 
+    for load in small[1:]:
+        load.wait()
     ids = ids_ref[...].astype(f32)
     ids_column = column_of(ids, iota((share, share), 0) == iota((share, share), 1))
     vocabulary = id_weight_ref.shape[1]
@@ -869,7 +890,6 @@
         teacher_width=F * T,
         scale=1.0 / math.sqrt(EP_LEN * E * O),
     )
-    vmem = pl.BlockSpec(memory_space=pltpu.VMEM)
     anywhere = pl.BlockSpec(memory_space=pl.ANY)
     DMA = pltpu.SemaphoreType.DMA
     scratch = [
@@ -908,7 +928,13 @@
         pltpu.VMEM((rows, W), bf16),
         pltpu.VMEM((O * out_rows, W), bf16),
         pltpu.VMEM((out_rows, DS), bf16),
-        DMA((6,)),
+        pltpu.VMEM((DS // 128, 128), f32),
+        pltpu.VMEM((1, E), jnp.int32),
+        pltpu.VMEM((1, share), jnp.int32),
+        pltpu.VMEM((1, E), jnp.int32),
+        pltpu.VMEM((1, id_weight.shape[0]), f32),
+        pltpu.VMEM((1, F), f32),
+        DMA((12,)),
         *[DMA((3,)) for _ in range(10)],
         *[DMA((T,)) for _ in range(2)],
         *[DMA((2, T)) for _ in range(4)],
@@ -926,7 +952,7 @@
             jax.ShapeDtypeStruct((out_rows, DS), bf16),
             jax.ShapeDtypeStruct((H, W), f32),
         ),
-        in_specs=[anywhere, vmem, anywhere, anywhere, vmem, anywhere, anywhere, anywhere, vmem, vmem, vmem, vmem],
+        in_specs=[anywhere] * 12,
         out_specs=(anywhere, anywhere, anywhere, anywhere),
         scratch_shapes=scratch,
         compiler_params=pltpu.CompilerParams(

time: 99.6 us -> 98.8 us (level)
  no operation moved by 1% of the time
where the time goes in v4:
time: 98.8 us; the launch traced here: 98.6 us
  Pallas kernels  98 us (99%)
    pallas_call x1, Pallas kernels, fused(): pl.pallas_call(functools.partial(fused_kernel, size), out_shape=(jax.Shap...  93.2 us
    pallas_call x1, Pallas kernels, fused(): pl.pallas_call(last_terms, out_shape=(jax.ShapeDtypeStruct((H, W), f32),...  4.75 us

profile of v4, /device:TPU:0, one launch (start us, length us, event | category | flops | bytes accessed | tf_op | source)
XLA Modules:
  0.0 98.6 jit_solution(2805123113638575757)
XLA Ops:
  0.6 93.2 %shard_map.131 = (bf16[128,896]{1,0:T(8,128)(2,1)}, bf16[1184,128]{1,0:T(8,128)(2,1)}, bf16[64,3584]{1,0:T(8,128)(2,1)}, f32[1184,896]{1,0:T(8,128)}) custom-call(bf16[256,1024]{1,0:T(8,128)(2,1)} %teacher_ref.1, f32[1,1024]{1,0:T(1,128)} %bitcast.13, bf16[1024,3584]{1,0:T(8,128)(2,1)} %project_ref.1, bf16[32,3584]{1,0:T(8,128)(2,1)} %student_ref.1, ...), custom_call_target="tpu_custom_call" | custom-call | tf_op jit(solution)/shard_map/pallas_call | solution.py:947
  93.9 4.7 %shard_map.132 = (f32[1184,896]{1,0:T(8,128)}, bf16[64,3584]{1,0:T(8,128)(2,1)}) custom-call(f32[1184,896]{1,0:T(8,128)} %get-tuple-element.8.sum_ref, bf16[1184,128]{1,0:T(8,128)(2,1)} %get-tuple-element.9.act_ref, bf16[128,896]{1,0:T(8,128)(2,1)} %get-tuple-element.10.grad_ref, bf16[64,3584]{1,0:T(8,128)(2,1)} %get-tuple-element.11.student_ref), custom_call_target="tpu_custom_call" | custom-call | tf_op jit(solution)/shard_map/pallas_call | solution.py:976
